TPU v7x, 32 devices: a whole 2x2x4 slice. The times are simulated.
32 devices in a mesh: row: 4 (over y, core), col: 8 (over z, x).
Axes of the slice: x: 2, y: 2, z: 4, core: 2. Of those that a mesh axis runs over, the one named last changes fastest.
Arguments:
- nodes: bfloat16 [32768, 512], P(('row', 'col')), may hold values from -8 to 8
- ln1_gain: float32 [512], replicated, may hold values from 0.25 to 1.75
- w_qkv: bfloat16 [512, 1536], replicated, may hold values from -1 to 1
- w_out: bfloat16 [512, 512], replicated, may hold values from -0.25 to 0.25
- ln2_gain: float32 [512], replicated, may hold values from 0.25 to 1.75
- w_up: bfloat16 [512, 2048], replicated, may hold values from -0.25 to 0.25
- w_down: bfloat16 [2048, 512], replicated, may hold values from -0.125 to 0.125
- adjacency: int32 [32768, 128], P(('row', 'col')), may hold values 0 or 1
- remote_ids: int32 [32, 10], replicated, may hold values from 0 to 255, as said below
- remote_live: int32 [32, 10], replicated, may hold values from 0 to 1, as said below
Outputs:
- updated: bfloat16 [32768, 512], P(('row', 'col'))
Inputs may be any that keep to these rules, and one draw needn't show every extreme that they name: `remote_ids`: every entry of device d's list names a block of another device in d's row or d's column of the mesh; the entries of one list are distinct; at most 1 live entries of one list name blocks of one device, and some list has exactly 1 from one device. `remote_live`: some device has all 10 entries live; every device has 8 or more.
All inputs are finite; a program needn't handle non-finite values. No bound on the sum of `adjacency` on one device may be relied on, other than what follows from the above.
Results may differ from a plain program's by a relative error of at most 0.005.
Values may be sent and summed in bfloat16 or wider, within the bound.
A program may use at most 128 MiB of HBM per device.

v0:
```python
import math
import jax
import jax.numpy as jnp
from jax import lax
from jax.sharding import PartitionSpec as P

HEADS = 8
BLK = 128
CAP = 1
EPS = 1e-05
NEG_FILL = -1e30


def normalize(values, gain):
    values = values.astype(jnp.float32)
    row_mean = jnp.mean(values, axis=-1, keepdims=True)
    centered = values - row_mean
    row_var = jnp.mean(centered * centered, axis=-1, keepdims=True)
    return (centered * lax.rsqrt(row_var + EPS) * gain).astype(jnp.bfloat16)


def attend(queries, local_kv, remote_kv, adj_rows, key_alive):
    row_count = queries.shape[0]
    model_width = queries.shape[1]
    head_dim = model_width // HEADS
    block_count = row_count // BLK
    score_scale = 1.0 / math.sqrt(head_dim)
    query_h = queries.reshape(block_count, BLK, HEADS, head_dim)
    local_keys = local_kv[:, :model_width].reshape(block_count, BLK, HEADS, head_dim)
    local_vals = local_kv[:, model_width:].reshape(block_count, BLK, HEADS, head_dim)
    remote_keys = remote_kv[:, :model_width].reshape(-1, HEADS, head_dim)
    remote_vals = remote_kv[:, model_width:].reshape(-1, HEADS, head_dim)
    local_scores = (
        jnp.einsum("bihd,bjhd->bhij", query_h, local_keys, preferred_element_type=jnp.float32)
        * score_scale
    )
    eye_mask = jnp.arange(BLK)[:, None] == jnp.arange(BLK)[None, :]
    allowed = (adj_rows.reshape(block_count, BLK, BLK) > 0) | eye_mask[None]
    local_scores = jnp.where(allowed[:, None], local_scores, NEG_FILL)
    remote_scores = (
        jnp.einsum("bihd,jhd->bhij", query_h, remote_keys, preferred_element_type=jnp.float32)
        * score_scale
    )
    remote_scores = jnp.where(key_alive[None, None, None, :] > 0, remote_scores, NEG_FILL)
    row_max = jnp.maximum(jnp.max(local_scores, axis=-1), jnp.max(remote_scores, axis=-1))
    local_exp = jnp.exp(local_scores - row_max[..., None])
    remote_exp = jnp.exp(remote_scores - row_max[..., None])
    row_total = jnp.sum(local_exp, axis=-1) + jnp.sum(remote_exp, axis=-1)
    local_probs = (local_exp / row_total[..., None]).astype(jnp.bfloat16)
    remote_probs = (remote_exp / row_total[..., None]).astype(jnp.bfloat16)
    summed = jnp.einsum(
        "bhij,bjhd->bihd", local_probs, local_vals, preferred_element_type=jnp.float32
    )
    summed = summed + jnp.einsum(
        "bhij,jhd->bihd", remote_probs, remote_vals, preferred_element_type=jnp.float32
    )
    return summed.reshape(row_count, model_width).astype(jnp.bfloat16)


def choose_blocks(owner_rows, rank_rows, alive_rows, local_rows, self_index):
    cap_iota = jnp.arange(CAP, dtype=jnp.int32)
    matched = (
        alive_rows[:, None, :]
        & (owner_rows[:, None, :] == self_index)
        & (rank_rows[:, None, :] == cap_iota[None, :, None])
    )
    return jnp.sum(matched.astype(jnp.int32) * local_rows[:, None, :], axis=2)


def outgoing(source, chosen_local, peer_count):
    picked = jnp.take(source, chosen_local.reshape(-1), axis=0, mode="clip")
    return picked.reshape(peer_count, CAP, BLK, source.shape[2])


def shards(
    nodes, ln1_gain, w_qkv, w_out, ln2_gain, w_up, w_down, adjacency, remote_ids, remote_live
):
    model_width = nodes.shape[1]
    node_count = nodes.shape[0]
    local_blocks = node_count // BLK
    slot_count = remote_ids.shape[1]
    row_size = lax.axis_size("row")
    col_size = lax.axis_size("col")
    my_row = lax.axis_index("row")
    my_col = lax.axis_index("col")
    self_index = my_row * col_size + my_col
    normed = normalize(nodes, ln1_gain)
    projected = jnp.dot(normed, w_qkv, preferred_element_type=jnp.float32).astype(jnp.bfloat16)
    queries = projected[:, :model_width]
    keyval = projected[:, model_width:]
    owner_dev = remote_ids // local_blocks
    local_slot = remote_ids % local_blocks
    alive_all = remote_live > 0
    same_owner = owner_dev[:, :, None] == owner_dev[:, None, :]
    slot_iota = jnp.arange(slot_count, dtype=jnp.int32)
    earlier = slot_iota[:, None] < slot_iota[None, :]
    slot_rank = jnp.sum(
        (same_owner & earlier[None] & alive_all[:, :, None]).astype(jnp.int32), axis=1
    )
    row_start = my_row * col_size
    col_pick = choose_blocks(
        lax.dynamic_slice_in_dim(owner_dev, row_start, col_size, 0),
        lax.dynamic_slice_in_dim(slot_rank, row_start, col_size, 0),
        lax.dynamic_slice_in_dim(alive_all, row_start, col_size, 0),
        lax.dynamic_slice_in_dim(local_slot, row_start, col_size, 0),
        self_index,
    )

    def column_of(table):
        return lax.dynamic_index_in_dim(
            table.reshape(row_size, col_size, slot_count), my_col, 1, keepdims=False
        )

    row_pick = choose_blocks(
        column_of(owner_dev),
        column_of(slot_rank),
        column_of(alive_all),
        column_of(local_slot),
        self_index,
    )
    source = normed.reshape(local_blocks, BLK, model_width)
    col_recv = lax.all_to_all(
        outgoing(source, col_pick, col_size), "col", split_axis=0, concat_axis=0, tiled=True
    )
    row_recv = lax.all_to_all(
        outgoing(source, row_pick, row_size), "row", split_axis=0, concat_axis=0, tiled=True
    )
    own_owner = lax.dynamic_index_in_dim(owner_dev, self_index, 0, keepdims=False)
    own_rank = jnp.minimum(
        lax.dynamic_index_in_dim(slot_rank, self_index, 0, keepdims=False), CAP - 1
    )
    own_alive = lax.dynamic_index_in_dim(remote_live, self_index, 0, keepdims=False)
    owner_row = own_owner // col_size
    owner_col = own_owner % col_size
    feature_width = col_recv.shape[3]
    from_col = jnp.take(
        col_recv.reshape(col_size * CAP, BLK, feature_width),
        owner_col * CAP + own_rank,
        axis=0,
        mode="clip",
    )
    from_row = jnp.take(
        row_recv.reshape(row_size * CAP, BLK, feature_width),
        owner_row * CAP + own_rank,
        axis=0,
        mode="clip",
    )
    gathered = jnp.where((owner_row == my_row)[:, None, None], from_col, from_row).reshape(
        slot_count * BLK, feature_width
    )
    remote_kv = jnp.dot(
        gathered, w_qkv[:, model_width:], preferred_element_type=jnp.float32
    ).astype(jnp.bfloat16)
    key_alive = jnp.repeat(own_alive, BLK)
    group_rows = 2 * BLK
    group_count = node_count // group_rows

    def one_group(pieces):
        query_part, kv_part, adj_part = pieces
        return attend(query_part, kv_part, remote_kv, adj_part, key_alive)

    mixed = lax.map(
        one_group,
        (
            queries.reshape(group_count, group_rows, model_width),
            keyval.reshape(group_count, group_rows, 2 * model_width),
            adjacency.reshape(group_count, group_rows, BLK),
        ),
    )
    mixed = mixed.reshape(node_count, model_width)
    residual = nodes.astype(jnp.float32) + jnp.dot(mixed, w_out, preferred_element_type=jnp.float32)
    normed_two = normalize(residual, ln2_gain)
    upward = jnp.dot(normed_two, w_up, preferred_element_type=jnp.float32)
    activated = jax.nn.gelu(upward, approximate=True).astype(jnp.bfloat16)
    return (residual + jnp.dot(activated, w_down, preferred_element_type=jnp.float32)).astype(
        jnp.bfloat16
    )


def solution(mesh):
    return jax.shard_map(
        shards,
        mesh=mesh,
        in_specs=(
            P(("row", "col"), None),
            P(),
            P(),
            P(),
            P(),
            P(),
            P(),
            P(("row", "col"), None),
            P(),
            P(),
        ),
        out_specs=P(("row", "col"), None),
        check_vma=False,
    )
```

profile of v0, /device:TPU:0, one launch (start us, length us, event | category | flops | bytes accessed | tf_op | source)
XLA Modules:
  0.0 227.4 jit_solution(1038354618828412443)
XLA Ops:
  9.1 4.3 %all-to-all-start.1 = ((bf16[4,1,128,512]{3,2,1,0:T(8,128)(2,1)}), bf16[4,1,128,512]{3,2,1,0:T(8,128)(2,1)}, u32[]{:S(2)}, u32[]{:S(2)}) async-start(bf16[4,1,128,512]{3,2,1,0:T(8,128)(2,1)} %bitcast.137), calls=%async_computation.1 | async-start | bytes 1048576 | tf_op jit(solution)/shard_map/all_to_all | solution.py:125
  15.1 7.7 %all-to-all-done.1 = bf16[4,1,128,512]{3,2,1,0:T(8,128)(2,1)} async-done(((bf16[4,1,128,512]{3,2,1,0:T(8,128)(2,1)}), bf16[4,1,128,512]{3,2,1,0:T(8,128)(2,1)}, u32[]{:S(2)}, u32[]{:S(2)}) %all-to-all-start.1) | async-done | bytes 524320 | tf_op jit(solution)/shard_map/all_to_all | solution.py:125
  22.9 6.6 %all-to-all-start = ((bf16[8,1,128,512]{3,2,1,0:T(8,128)(2,1)}), bf16[8,1,128,512]{3,2,1,0:T(8,128)(2,1)S(1)}, u32[]{:S(2)}, u32[]{:S(2)}) async-start(bf16[8,1,128,512]{3,2,1,0:T(8,128)(2,1)} %bitcast.135), calls=%async_computation | async-start | bytes 2097152 | tf_op jit(solution)/shard_map/all_to_all | solution.py:122
  29.4 3.6 %convolution_convert_fusion.1 = bf16[1024,1536]{1,0:T(8,128)(2,1)S(1)} fusion(bf16[1024,512]{0,1:T(8,128)(2,1)} %fusion.34, bf16[512,1536]{1,0:T(8,128)(2,1)} %param.14), kind=kOutput, calls=%fused_computation.50 | convolution fusion | flops 1612185600 | bytes 5767168 | tf_op jit(solution)/shard_map/dot_general | solution.py:88
  39.0 16.1 %all-to-all-done = bf16[8,1,128,512]{3,2,1,0:T(8,128)(2,1)S(1)} async-done(((bf16[8,1,128,512]{3,2,1,0:T(8,128)(2,1)}), bf16[8,1,128,512]{3,2,1,0:T(8,128)(2,1)S(1)}, u32[]{:S(2)}, u32[]{:S(2)}) %all-to-all-start) | async-done | bytes 1048608 | tf_op jit(solution)/shard_map/all_to_all | solution.py:122
  59.0 3.0 %convolution_convert_fusion = bf16[1280,1024]{1,0:T(8,128)(2,1)} fusion(bf16[1280,512]{1,0:T(8,128)(2,1)S(1)} %bitcast_select_fusion, bf16[512,1536]{1,0:T(8,128)(2,1)S(1)} %copy-done.11), kind=kOutput, calls=%fused_computation.49 | convolution fusion | flops 1343488000 | bytes 4980736 | tf_op jit(solution)/shard_map/dot_general | solution.py:151
  62.0 4.4 %copy.136 = bf16[1280,1024]{0,1:T(8,128)(2,1)} copy(bf16[1280,1024]{1,0:T(8,128)(2,1)} %convolution_convert_fusion) | data formatting | bytes 5242880
  66.5 147.2 %while.11 = (s32[]{:T(128)}, bf16[4,256,512]{2,1,0:T(8,128)(2,1)}, bf16[4,256,1024]{2,1,0:T(8,128)(2,1)}, s32[4,256,128]{2,1,0:T(8,128)}, bf16[4,256,512]{2,1,0:...) while((s32[]{:T(128)}, bf16[4,256,512]{2,1,0:T(8,128)(2,1)}, ...), condition=%wide.region_10.11_spmd.clone, body=%wide.region_5.10_spmd.clone.sunk | while | flops 772091904 | bytes 101979416 | solution.py:162
  66.5 3.0 %fusion.88 = (bf16[1280,512]{0,1:T(8,128)(2,1)S(1)}, bf16[1280,512]{0,1:T(8,128)(2,1)}) fusion(bf16[1280,1024]{0,1:T(8,128)(2,1)} %get-tuple-element.212), kind=kLoop, calls=%fused_computation.120.clone.1 | loop fusion | bytes 5242880 | tf_op jit(solution)/shard_map/while/body/eval_jaxpr/slice | solution.py:31
  74.7 6.5 %bitcast_reduce_fusion.2 = (f32[2,8,128]{2,0,1:T(2,128)S(1)}, f32[8,2,128,1280]{3,2,1,0:T(8,128)}) fusion(pred[1280]{0:T(1024)(128)(4,1)S(1)} %broadcast_bitcast_fusion.3, bf16[1280,8,64,1]{0,2,3,1:T(8,128)(2,1)S(1)} %bitcast.127, bf16[2,128,8,64]{1,0,3,2:T(2,128)(2,1)} %reshape.378), kind=kOutput, calls=%fused_computation.6.clone.1 | convolution fusion | flops 343406592 | bytes 12068096 | tf_op jit(solution)/shard_map/while/body/eval_jaxpr/bihd,jhd->bhij/dot_general | solution.py:41
  86.8 6.4 %fusion.92 = f32[2,8,128]{2,0,1:T(2,128)S(1)} fusion(f32[8,2,128,1280]{3,2,1,0:T(8,128)} %get-tuple-element.185, f32[2,8,128]{2,0,1:T(2,128)S(1)} %copy.193, pred[1280]{0:T(1024)(128)(4,1)S(1)} %broadcast_bitcast_fusion.3), kind=kLoop, calls=%fused_computation.10.clone.1 | loop fusion | flops 10483712 | bytes 10503424 | tf_op jit(solution)/shard_map/while/body/eval_jaxpr/reduce_sum | solution.py:48
  93.8 4.2 %fusion.93 = f32[2,128,8,64]{1,3,2,0:T(8,128)} fusion(bf16[1280,8,64,1]{0,2,1,3:T(8,128)(2,1)S(1)} %bitcast.129, f32[8,2,128,1280]{3,2,1,0:T(8,128)S(1)} %copy-done.1, f32[2,8,128]{2,0,1:T(2,128)S(1)} %copy.194, f32[2,8,128]{2,0,1:T(2,128)S(1)} %copy.193, pred[1280]{0:T(1024)(128)(4,1)S(1)} %broadcast_bitcast_fusion.3), kind=kOutput, calls=%fused_computation.15.clone.1 | convolution fusion | flops 348651520 | bytes 12338432 | tf_op jit(solution)/shard_map/while/body/eval_jaxpr/bhij,jhd->bihd/dot_general | solution.py:54
  103.3 3.0 %fusion.88 = (bf16[1280,512]{0,1:T(8,128)(2,1)S(1)}, bf16[1280,512]{0,1:T(8,128)(2,1)}) fusion(bf16[1280,1024]{0,1:T(8,128)(2,1)} %get-tuple-element.212), kind=kLoop, calls=%fused_computation.120.clone.1 | loop fusion | bytes 5242880 | tf_op jit(solution)/shard_map/while/body/eval_jaxpr/slice | solution.py:31
  111.5 6.5 %bitcast_reduce_fusion.2 = (f32[2,8,128]{2,0,1:T(2,128)S(1)}, f32[8,2,128,1280]{3,2,1,0:T(8,128)}) fusion(pred[1280]{0:T(1024)(128)(4,1)S(1)} %broadcast_bitcast_fusion.3, bf16[1280,8,64,1]{0,2,3,1:T(8,128)(2,1)S(1)} %bitcast.127, bf16[2,128,8,64]{1,0,3,2:T(2,128)(2,1)} %reshape.378), kind=kOutput, calls=%fused_computation.6.clone.1 | convolution fusion | flops 343406592 | bytes 12068096 | tf_op jit(solution)/shard_map/while/body/eval_jaxpr/bihd,jhd->bhij/dot_general | solution.py:41
  123.6 6.4 %fusion.92 = f32[2,8,128]{2,0,1:T(2,128)S(1)} fusion(f32[8,2,128,1280]{3,2,1,0:T(8,128)} %get-tuple-element.185, f32[2,8,128]{2,0,1:T(2,128)S(1)} %copy.193, pred[1280]{0:T(1024)(128)(4,1)S(1)} %broadcast_bitcast_fusion.3), kind=kLoop, calls=%fused_computation.10.clone.1 | loop fusion | flops 10483712 | bytes 10503424 | tf_op jit(solution)/shard_map/while/body/eval_jaxpr/reduce_sum | solution.py:48
  130.6 4.2 %fusion.93 = f32[2,128,8,64]{1,3,2,0:T(8,128)} fusion(bf16[1280,8,64,1]{0,2,1,3:T(8,128)(2,1)S(1)} %bitcast.129, f32[8,2,128,1280]{3,2,1,0:T(8,128)S(1)} %copy-done.1, f32[2,8,128]{2,0,1:T(2,128)S(1)} %copy.194, f32[2,8,128]{2,0,1:T(2,128)S(1)} %copy.193, pred[1280]{0:T(1024)(128)(4,1)S(1)} %broadcast_bitcast_fusion.3), kind=kOutput, calls=%fused_computation.15.clone.1 | convolution fusion | flops 348651520 | bytes 12338432 | tf_op jit(solution)/shard_map/while/body/eval_jaxpr/bhij,jhd->bihd/dot_general | solution.py:54
  148.3 6.5 %bitcast_reduce_fusion.2 = (f32[2,8,128]{2,0,1:T(2,128)S(1)}, f32[8,2,128,1280]{3,2,1,0:T(8,128)}) fusion(pred[1280]{0:T(1024)(128)(4,1)S(1)} %broadcast_bitcast_fusion.3, bf16[1280,8,64,1]{0,2,3,1:T(8,128)(2,1)S(1)} %bitcast.127, bf16[2,128,8,64]{1,0,3,2:T(2,128)(2,1)} %reshape.378), kind=kOutput, calls=%fused_computation.6.clone.1 | convolution fusion | flops 343406592 | bytes 12068096 | tf_op jit(solution)/shard_map/while/body/eval_jaxpr/bihd,jhd->bhij/dot_general | solution.py:41
  160.4 6.4 %fusion.92 = f32[2,8,128]{2,0,1:T(2,128)S(1)} fusion(f32[8,2,128,1280]{3,2,1,0:T(8,128)} %get-tuple-element.185, f32[2,8,128]{2,0,1:T(2,128)S(1)} %copy.193, pred[1280]{0:T(1024)(128)(4,1)S(1)} %broadcast_bitcast_fusion.3), kind=kLoop, calls=%fused_computation.10.clone.1 | loop fusion | flops 10483712 | bytes 10503424 | tf_op jit(solution)/shard_map/while/body/eval_jaxpr/reduce_sum | solution.py:48
  167.4 4.2 %fusion.93 = f32[2,128,8,64]{1,3,2,0:T(8,128)} fusion(bf16[1280,8,64,1]{0,2,1,3:T(8,128)(2,1)S(1)} %bitcast.129, f32[8,2,128,1280]{3,2,1,0:T(8,128)S(1)} %copy-done.1, f32[2,8,128]{2,0,1:T(2,128)S(1)} %copy.194, f32[2,8,128]{2,0,1:T(2,128)S(1)} %copy.193, pred[1280]{0:T(1024)(128)(4,1)S(1)} %broadcast_bitcast_fusion.3), kind=kOutput, calls=%fused_computation.15.clone.1 | convolution fusion | flops 348651520 | bytes 12338432 | tf_op jit(solution)/shard_map/while/body/eval_jaxpr/bhij,jhd->bihd/dot_general | solution.py:54
  176.8 3.0 %fusion.88 = (bf16[1280,512]{0,1:T(8,128)(2,1)S(1)}, bf16[1280,512]{0,1:T(8,128)(2,1)}) fusion(bf16[1280,1024]{0,1:T(8,128)(2,1)} %get-tuple-element.212), kind=kLoop, calls=%fused_computation.120.clone.1 | loop fusion | bytes 5242880 | tf_op jit(solution)/shard_map/while/body/eval_jaxpr/slice | solution.py:31
  185.1 6.5 %bitcast_reduce_fusion.2 = (f32[2,8,128]{2,0,1:T(2,128)S(1)}, f32[8,2,128,1280]{3,2,1,0:T(8,128)}) fusion(pred[1280]{0:T(1024)(128)(4,1)S(1)} %broadcast_bitcast_fusion.3, bf16[1280,8,64,1]{0,2,3,1:T(8,128)(2,1)S(1)} %bitcast.127, bf16[2,128,8,64]{1,0,3,2:T(2,128)(2,1)} %reshape.378), kind=kOutput, calls=%fused_computation.6.clone.1 | convolution fusion | flops 343406592 | bytes 12068096 | tf_op jit(solution)/shard_map/while/body/eval_jaxpr/bihd,jhd->bhij/dot_general | solution.py:41
  197.2 6.4 %fusion.92 = f32[2,8,128]{2,0,1:T(2,128)S(1)} fusion(f32[8,2,128,1280]{3,2,1,0:T(8,128)} %get-tuple-element.185, f32[2,8,128]{2,0,1:T(2,128)S(1)} %copy.193, pred[1280]{0:T(1024)(128)(4,1)S(1)} %broadcast_bitcast_fusion.3), kind=kLoop, calls=%fused_computation.10.clone.1 | loop fusion | flops 10483712 | bytes 10503424 | tf_op jit(solution)/shard_map/while/body/eval_jaxpr/reduce_sum | solution.py:48
  204.2 4.2 %fusion.93 = f32[2,128,8,64]{1,3,2,0:T(8,128)} fusion(bf16[1280,8,64,1]{0,2,1,3:T(8,128)(2,1)S(1)} %bitcast.129, f32[8,2,128,1280]{3,2,1,0:T(8,128)S(1)} %copy-done.1, f32[2,8,128]{2,0,1:T(2,128)S(1)} %copy.194, f32[2,8,128]{2,0,1:T(2,128)S(1)} %copy.193, pred[1280]{0:T(1024)(128)(4,1)S(1)} %broadcast_bitcast_fusion.3), kind=kOutput, calls=%fused_computation.15.clone.1 | convolution fusion | flops 348651520 | bytes 12338432 | tf_op jit(solution)/shard_map/while/body/eval_jaxpr/bhij,jhd->bihd/dot_general | solution.py:54
  217.8 8.3 %add_convert_fusion = bf16[1024,512]{0,1:T(8,128)(2,1)S(1)} fusion(f32[1024,512]{0,1:T(8,128)} %copy-done.6, bf16[2048,512]{1,0:T(8,128)(2,1)S(1)} %copy-done, bf16[512,2048]{1,0:T(8,128)(2,1)} %param.17, f32[512]{0:T(512)S(1)} %copy-done.12, f32[1024]{0:T(1024)S(1)} %add_rsqrt_fusion, f32[1024]{0:T(1024)S(1)} %broadcast_multiply_fusion), kind=kOutput, calls=%fused_computation.59 | convolution fusion | flops 4316987392 | bytes 7350272 | tf_op jit(solution)/shard_map/dot_general | solution.py:175
  (186 shorter events, 95.3 us)
Async XLA Ops:
  0.0 217.8 %copy-start = (bf16[2048,512]{1,0:T(8,128)(2,1)S(1)}, bf16[2048,512]{1,0:T(8,128)(2,1)}, u32[]{:S(2)}) copy-start(bf16[2048,512]{1,0:T(8,128)(2,1)} %param.18) | copy-start | bytes 6291460
  0.0 2.2 copy-start.10
  2.2 3.6 %copy-start.9 = (s32[32,10]{0,1:T(8,128)S(1)}, s32[32,10]{0,1:T(8,128)}, u32[]{:S(2)}) copy-start(s32[32,10]{0,1:T(8,128)} %param.20) | copy-start | bytes 3844
  2.2 3.8 %copy-start.8 = (s32[32,10]{0,1:T(8,128)S(1)}, s32[32,10]{0,1:T(8,128)}, u32[]{:S(2)}) copy-start(s32[32,10]{0,1:T(8,128)} %param.21) | copy-start | bytes 3844
  5.8 7.7 %copy-start.7 = (bf16[1024,512]{1,0:T(8,128)(2,1)S(1)}, bf16[1024,512]{1,0:T(8,128)(2,1)}, u32[]{:S(2)}) copy-start(bf16[1024,512]{1,0:T(8,128)(2,1)} %copy.143) | copy-start | bytes 3145732
  9.1 13.7 %all-to-all-start.1 = ((bf16[4,1,128,512]{3,2,1,0:T(8,128)(2,1)}), bf16[4,1,128,512]{3,2,1,0:T(8,128)(2,1)}, u32[]{:S(2)}, u32[]{:S(2)}) async-start(bf16[4,1,128,512]{3,2,1,0:T(8,128)(2,1)} %bitcast.137), calls=%async_computation.1 | async-start | bytes 1048576 | tf_op jit(solution)/shard_map/all_to_all | solution.py:125
  22.9 32.2 %all-to-all-start = ((bf16[8,1,128,512]{3,2,1,0:T(8,128)(2,1)}), bf16[8,1,128,512]{3,2,1,0:T(8,128)(2,1)S(1)}, u32[]{:S(2)}, u32[]{:S(2)}) async-start(bf16[8,1,128,512]{3,2,1,0:T(8,128)(2,1)} %bitcast.135), calls=%async_computation | async-start | bytes 2097152 | tf_op jit(solution)/shard_map/all_to_all | solution.py:122
  56.8 2.2 copy-start.11
  81.2 4.0 %copy-start.2 = (bf16[2,128,8,64]{1,0,3,2:T(2,128)(2,1)S(1)}, bf16[2,128,8,64]{1,0,3,2:T(2,128)(2,1)}, u32[]{:S(2)}) copy-start(bf16[2,128,8,64]{1,0,3,2:T(2,128)(2,1)} %reshape.378) | copy-start | bytes 786436 | tf_op jit(solution)/shard_map/while
  85.2 8.0 %copy-start.3 = (bf16[1280,512]{0,1:T(8,128)(2,1)S(1)}, bf16[1280,512]{0,1:T(8,128)(2,1)}, u32[]{:S(2)}) copy-start(bf16[1280,512]{0,1:T(8,128)(2,1)} %get-tuple-element.183) | copy-start | bytes 3932164 | tf_op jit(solution)/shard_map/while
  86.8 7.0 %copy-start.1 = (f32[8,2,128,1280]{3,2,1,0:T(8,128)S(1)}, f32[8,2,128,1280]{3,2,1,0:T(8,128)}, u32[]{:S(2)}) copy-start(f32[8,2,128,1280]{3,2,1,0:T(8,128)} %get-tuple-element.185) | copy-start | bytes 31457284 | tf_op jit(solution)/shard_map/while
  93.8 4.2 %copy-start.5 = (bf16[256,512]{0,1:T(8,128)(2,1)S(1)}, bf16[256,512]{0,1:T(8,128)(2,1)}, u32[]{:S(2)}) copy-start(bf16[256,512]{0,1:T(8,128)(2,1)} %get-tuple-element.190) | copy-start | bytes 786436 | tf_op jit(solution)/shard_map/while
  118.0 4.0 %copy-start.2 = (bf16[2,128,8,64]{1,0,3,2:T(2,128)(2,1)S(1)}, bf16[2,128,8,64]{1,0,3,2:T(2,128)(2,1)}, u32[]{:S(2)}) copy-start(bf16[2,128,8,64]{1,0,3,2:T(2,128)(2,1)} %reshape.378) | copy-start | bytes 786436 | tf_op jit(solution)/shard_map/while
  122.0 8.1 %copy-start.3 = (bf16[1280,512]{0,1:T(8,128)(2,1)S(1)}, bf16[1280,512]{0,1:T(8,128)(2,1)}, u32[]{:S(2)}) copy-start(bf16[1280,512]{0,1:T(8,128)(2,1)} %get-tuple-element.183) | copy-start | bytes 3932164 | tf_op jit(solution)/shard_map/while
  123.6 7.0 %copy-start.1 = (f32[8,2,128,1280]{3,2,1,0:T(8,128)S(1)}, f32[8,2,128,1280]{3,2,1,0:T(8,128)}, u32[]{:S(2)}) copy-start(f32[8,2,128,1280]{3,2,1,0:T(8,128)} %get-tuple-element.185) | copy-start | bytes 31457284 | tf_op jit(solution)/shard_map/while
  130.6 4.2 %copy-start.5 = (bf16[256,512]{0,1:T(8,128)(2,1)S(1)}, bf16[256,512]{0,1:T(8,128)(2,1)}, u32[]{:S(2)}) copy-start(bf16[256,512]{0,1:T(8,128)(2,1)} %get-tuple-element.190) | copy-start | bytes 786436 | tf_op jit(solution)/shard_map/while
  154.8 4.0 %copy-start.2 = (bf16[2,128,8,64]{1,0,3,2:T(2,128)(2,1)S(1)}, bf16[2,128,8,64]{1,0,3,2:T(2,128)(2,1)}, u32[]{:S(2)}) copy-start(bf16[2,128,8,64]{1,0,3,2:T(2,128)(2,1)} %reshape.378) | copy-start | bytes 786436 | tf_op jit(solution)/shard_map/while
  158.8 8.1 %copy-start.3 = (bf16[1280,512]{0,1:T(8,128)(2,1)S(1)}, bf16[1280,512]{0,1:T(8,128)(2,1)}, u32[]{:S(2)}) copy-start(bf16[1280,512]{0,1:T(8,128)(2,1)} %get-tuple-element.183) | copy-start | bytes 3932164 | tf_op jit(solution)/shard_map/while
  160.4 7.0 %copy-start.1 = (f32[8,2,128,1280]{3,2,1,0:T(8,128)S(1)}, f32[8,2,128,1280]{3,2,1,0:T(8,128)}, u32[]{:S(2)}) copy-start(f32[8,2,128,1280]{3,2,1,0:T(8,128)} %get-tuple-element.185) | copy-start | bytes 31457284 | tf_op jit(solution)/shard_map/while
  167.4 4.2 %copy-start.5 = (bf16[256,512]{0,1:T(8,128)(2,1)S(1)}, bf16[256,512]{0,1:T(8,128)(2,1)}, u32[]{:S(2)}) copy-start(bf16[256,512]{0,1:T(8,128)(2,1)} %get-tuple-element.190) | copy-start | bytes 786436 | tf_op jit(solution)/shard_map/while
  191.6 4.0 %copy-start.2 = (bf16[2,128,8,64]{1,0,3,2:T(2,128)(2,1)S(1)}, bf16[2,128,8,64]{1,0,3,2:T(2,128)(2,1)}, u32[]{:S(2)}) copy-start(bf16[2,128,8,64]{1,0,3,2:T(2,128)(2,1)} %reshape.378) | copy-start | bytes 786436 | tf_op jit(solution)/shard_map/while
  195.6 8.1 %copy-start.3 = (bf16[1280,512]{0,1:T(8,128)(2,1)S(1)}, bf16[1280,512]{0,1:T(8,128)(2,1)}, u32[]{:S(2)}) copy-start(bf16[1280,512]{0,1:T(8,128)(2,1)} %get-tuple-element.183) | copy-start | bytes 3932164 | tf_op jit(solution)/shard_map/while
  197.2 7.0 %copy-start.1 = (f32[8,2,128,1280]{3,2,1,0:T(8,128)S(1)}, f32[8,2,128,1280]{3,2,1,0:T(8,128)}, u32[]{:S(2)}) copy-start(f32[8,2,128,1280]{3,2,1,0:T(8,128)} %get-tuple-element.185) | copy-start | bytes 31457284 | tf_op jit(solution)/shard_map/while
  204.2 4.2 %copy-start.5 = (bf16[256,512]{0,1:T(8,128)(2,1)S(1)}, bf16[256,512]{0,1:T(8,128)(2,1)}, u32[]{:S(2)}) copy-start(bf16[256,512]{0,1:T(8,128)(2,1)} %get-tuple-element.190) | copy-start | bytes 786436 | tf_op jit(solution)/shard_map/while
  (3 other events, 4.9 us)
where the time goes:
time: 229 us; the launch traced here: 227 us
  local copies, waits for them, and re-layouts  82.4 us (36%)
  matrix products  74.7 us (33%)
  other arithmetic  35 us (15%)
  waiting for transfers between devices  23.8 us (10%)
  starting transfers between devices  10.8 us (5%)
    dot_general x4, matrix products, attend(): jnp.einsum('bihd,jhd->bhij', query_h, remote_keys, preferred_element_type...  26.2 us
    reduce_sum x8, other arithmetic, attend(): row_total = jnp.sum(local_exp, axis=-1) + jnp.sum(remote_exp, axis=-1)  26.2 us
    dynamic_slice x16, local copies, waits for them, and re-layouts, shards(): lax.map(one_group, (queries.reshape(group_count, group_rows, model_width)...  19.1 us
    dot_general x4, matrix products, attend(): jnp.einsum('bhij,jhd->bihd', remote_probs, remote_vals, preferred_element...  16.9 us
    all_to_all x1, waiting for transfers between devices, shards(): lax.all_to_all(outgoing(source, col_pick, col_size), 'col', split_axis=0,...  16.1 us
    slice x4, local copies, waits for them, and re-layouts, attend(): remote_keys = remote_kv[:, :model_width].reshape(-1, HEADS, head_dim)  11.9 us
    dynamic_update_slice x12, local copies, waits for them, and re-layouts, shards(): lax.map(one_group, (queries.reshape(group_count, group_rows, model_width)...  9.18 us
    dot_general x4, matrix products, attend(): jnp.einsum('bhij,bjhd->bihd', local_probs, local_vals, preferred_element_...  8.63 us
  transfers between devices with their start and end apart: 2, of which 2 were waited for; matrix products, arithmetic and copies ran while one was open for 5% of the time, Pallas kernels for 0%

commit v1 on v0

--- a/solution.py
+++ b/solution.py
@@ -9,6 +9,38 @@
 CAP = 1
 EPS = 1e-05
 NEG_FILL = -1e30
+
+
+def _put_cubes(obj, axis_k, local):
+    w2 = obj.shape
+    wide_out = obj.reshape(*w2[:axis_k], local, w2[axis_k] // local, *w2[axis_k + 1 :])
+    near = jnp.moveaxis(wide_out, axis_k, 0)
+    return near
+
+
+def spread_set_up(packet, which_dim):
+    packet = jnp.moveaxis(packet, 0, which_dim)
+    parts_out = packet.shape
+    big = packet.reshape(
+        *parts_out[:which_dim],
+        parts_out[which_dim] * parts_out[which_dim + 1],
+        *parts_out[which_dim + 2 :]
+    )
+    return big
+
+
+def group_the_set(incoming_x, a_name, mine, local_block):
+    z1, field_out = (lax.axis_size(a_name), lax.axis_index(a_name))
+    block_now = _put_cubes(incoming_x, mine, z1)
+    grid = [block_now[field_out]]
+    for u in range(1, z1):
+        work_now = block_now[field_out ^ u]
+        grid.append(
+            lax.ppermute(work_now, axis_name=a_name, perm=[(nth, nth ^ u) for nth in range(z1)])
+        )
+    block_now = jnp.stack(grid, 0)[field_out ^ jnp.arange(z1)]
+    res = spread_set_up(block_now, local_block)
+    return res
 
 
 def normalize(values, gain):
@@ -122,9 +154,7 @@
     col_recv = lax.all_to_all(
         outgoing(source, col_pick, col_size), "col", split_axis=0, concat_axis=0, tiled=True
     )
-    row_recv = lax.all_to_all(
-        outgoing(source, row_pick, row_size), "row", split_axis=0, concat_axis=0, tiled=True
-    )
+    row_recv = group_the_set(outgoing(source, row_pick, row_size), "row", 0, 0)
     own_owner = lax.dynamic_index_in_dim(owner_dev, self_index, 0, keepdims=False)
     own_rank = jnp.minimum(
         lax.dynamic_index_in_dim(slot_rank, self_index, 0, keepdims=False), CAP - 1

time: 229 us -> 217 us (0.948)
  waiting for transfers between devices: 23.8 us -> 7.29 us
  local copies, waits for them, and re-layouts: 82.4 us -> 87 us
    all_to_all x1, waiting for transfers between devices: 16.1 us -> 7.28 us  [shards(): lax.all_to_all(outgoing(source, col_pick, col_size), 'col', split_axis=0,...]
    all_to_all x1 -> x0, waiting for transfers between devices: 7.71 us -> none  [shards(): lax.all_to_all(outgoing(source, row_pick, row_size), 'row', split_axis=0,...]
    all_to_all x1 -> x0, starting transfers between devices: 4.27 us -> none  [shards(): lax.all_to_all(outgoing(source, row_pick, row_size), 'row', split_axis=0,...]
    unnamed x20 -> x22, local copies, waits for them, and re-layouts: 7.54 us -> 7.48 us
  transfers between devices with their start and end apart: 2 -> 4, of which waited for: 2 -> 1; matrix products, arithmetic and copies ran while one was open for 5% -> 8% of each run, Pallas kernels for 0% -> 0%
where the time goes in v1:
time: 217 us; the launch traced here: 215 us
  local copies, waits for them, and re-layouts  87 us (40%)
  matrix products  76.3 us (35%)
  other arithmetic  34.7 us (16%)
  starting transfers between devices  9.21 us (4%)
  waiting for transfers between devices  7.29 us (3%)
    dot_general x4, matrix products, attend(): jnp.einsum('bihd,jhd->bhij', query_h, remote_keys, preferred_element_type...  26.2 us
    reduce_sum x8, other arithmetic, attend(): row_total = jnp.sum(local_exp, axis=-1) + jnp.sum(remote_exp, axis=-1)  26.2 us
    dynamic_slice x16, local copies, waits for them, and re-layouts, shards(): lax.map(one_group, (queries.reshape(group_count, group_rows, model_width)...  19.1 us
    dot_general x4, matrix products, attend(): jnp.einsum('bhij,jhd->bihd', remote_probs, remote_vals, preferred_element...  16.9 us
    slice x4, local copies, waits for them, and re-layouts, attend(): remote_keys = remote_kv[:, :model_width].reshape(-1, HEADS, head_dim)  11.9 us
    dynamic_update_slice x12, local copies, waits for them, and re-layouts, shards(): lax.map(one_group, (queries.reshape(group_count, group_rows, model_width)...  9.18 us
    dot_general x4, matrix products, attend(): jnp.einsum('bhij,bjhd->bihd', local_probs, local_vals, preferred_element_...  8.63 us
    dot_general x1, matrix products, shards(): jnp.dot(activated, w_down, preferred_element_type=jnp.float32)  8.26 us
  transfers between devices with their start and end apart: 4, of which 1 were waited for; matrix products, arithmetic and copies ran while one was open for 8% of the time, Pallas kernels for 0%

profile of v1, /device:TPU:0, one launch (start us, length us, event | category | flops | bytes accessed | tf_op | source)
XLA Modules:
  0.0 215.3 jit_solution(11031788997186374682)
XLA Ops:
  9.0 7.3 %all-to-all-start = ((bf16[8,1,128,512]{3,2,1,0:T(8,128)(2,1)}), bf16[8,1,128,512]{3,2,1,0:T(8,128)(2,1)}, u32[]{:S(2)}, u32[]{:S(2)}) async-start(bf16[8,1,128,512]{3,2,1,0:T(8,128)(2,1)} %bitcast.145), calls=%async_computation | async-start | bytes 2097152 | tf_op jit(solution)/shard_map/all_to_all | solution.py:154
  21.6 5.2 %convolution_convert_fusion.1 = bf16[1024,1536]{1,0:T(8,128)(2,1)} fusion(bf16[1024,512]{0,1:T(8,128)(2,1)} %fusion.34, bf16[512,1536]{1,0:T(8,128)(2,1)} %param.14), kind=kOutput, calls=%fused_computation.51 | convolution fusion | flops 1612185600 | bytes 5767168 | tf_op jit(solution)/shard_map/dot_general | solution.py:120
  26.8 3.1 %slice.40 = bf16[1024,1024]{1,0:T(8,128)(2,1)} slice(bf16[1024,1536]{1,0:T(8,128)(2,1)} %convolution_convert_fusion.1), slice={[0:1024], [512:1536]} | slice | bytes 4194304 | tf_op jit(solution)/shard_map/slice | solution.py:122
  34.9 7.3 %all-to-all-done = bf16[8,1,128,512]{3,2,1,0:T(8,128)(2,1)} async-done(((bf16[8,1,128,512]{3,2,1,0:T(8,128)(2,1)}), bf16[8,1,128,512]{3,2,1,0:T(8,128)(2,1)}, u32[]{:S(2)}, u32[]{:S(2)}) %all-to-all-start) | async-done | bytes 1048608 | tf_op jit(solution)/shard_map/all_to_all | solution.py:154
  42.1 3.0 %gather_fusion.1 = bf16[10,128,512]{2,1,0:T(8,128)(2,1)} fusion(bf16[8,128,512]{2,1,0:T(8,128)(2,1)} %bitcast.6, s32[1024]{0:T(1024)S(1)} %pad_clamp_fusion.3), kind=kCustom, calls=%fused_computation.1 | custom fusion | bytes 2621480 | tf_op jit(solution)/shard_map/jit(_take)/gather | solution.py:166
  47.0 3.0 %convolution_convert_fusion = bf16[1280,1024]{1,0:T(8,128)(2,1)} fusion(bf16[1280,512]{1,0:T(8,128)(2,1)S(1)} %bitcast_select_fusion, bf16[512,1536]{1,0:T(8,128)(2,1)S(1)} %copy-done.12), kind=kOutput, calls=%fused_computation.50 | convolution fusion | flops 1343488000 | bytes 4980736 | tf_op jit(solution)/shard_map/dot_general | solution.py:181
  50.0 4.4 %copy.133 = bf16[1280,1024]{0,1:T(8,128)(2,1)} copy(bf16[1280,1024]{1,0:T(8,128)(2,1)} %convolution_convert_fusion) | data formatting | bytes 5242880
  54.4 147.2 %while.11 = (s32[]{:T(128)}, bf16[4,256,512]{2,1,0:T(8,128)(2,1)}, bf16[4,256,1024]{2,1,0:T(8,128)(2,1)}, s32[4,256,128]{2,1,0:T(8,128)}, bf16[4,256,512]{2,1,0:...) while((s32[]{:T(128)}, bf16[4,256,512]{2,1,0:T(8,128)(2,1)}, ...), condition=%wide.region_10.11_spmd.clone, body=%wide.region_5.10_spmd.clone.sunk | while | flops 772091904 | bytes 101979416 | solution.py:192
  54.4 3.0 %fusion.89 = (bf16[1280,512]{0,1:T(8,128)(2,1)S(1)}, bf16[1280,512]{0,1:T(8,128)(2,1)}) fusion(bf16[1280,1024]{0,1:T(8,128)(2,1)} %get-tuple-element.216), kind=kLoop, calls=%fused_computation.129.clone.1 | loop fusion | bytes 5242880 | tf_op jit(solution)/shard_map/while/body/eval_jaxpr/slice | solution.py:63
  62.6 6.5 %bitcast_reduce_fusion.2 = (f32[2,8,128]{2,0,1:T(2,128)S(1)}, f32[8,2,128,1280]{3,2,1,0:T(8,128)}) fusion(pred[1280]{0:T(1024)(128)(4,1)S(1)} %broadcast_bitcast_fusion.3, bf16[1280,8,64,1]{0,2,3,1:T(8,128)(2,1)S(1)} %bitcast.138, bf16[2,128,8,64]{1,0,3,2:T(2,128)(2,1)} %reshape.408), kind=kOutput, calls=%fused_computation.7.clone.1 | convolution fusion | flops 343406592 | bytes 12068096 | tf_op jit(solution)/shard_map/while/body/eval_jaxpr/bihd,jhd->bhij/dot_general | solution.py:73
  74.8 6.4 %fusion.93 = f32[2,8,128]{2,0,1:T(2,128)S(1)} fusion(f32[8,2,128,1280]{3,2,1,0:T(8,128)} %get-tuple-element.189, f32[2,8,128]{2,0,1:T(2,128)S(1)} %copy.190, pred[1280]{0:T(1024)(128)(4,1)S(1)} %broadcast_bitcast_fusion.3), kind=kLoop, calls=%fused_computation.11.clone.1 | loop fusion | flops 10483712 | bytes 10503424 | tf_op jit(solution)/shard_map/while/body/eval_jaxpr/reduce_sum | solution.py:80
  81.7 4.2 %fusion.94 = f32[2,128,8,64]{1,3,2,0:T(8,128)} fusion(bf16[1280,8,64,1]{0,2,1,3:T(8,128)(2,1)S(1)} %bitcast.140, f32[8,2,128,1280]{3,2,1,0:T(8,128)S(1)} %copy-done.1, f32[2,8,128]{2,0,1:T(2,128)S(1)} %copy.191, f32[2,8,128]{2,0,1:T(2,128)S(1)} %copy.190, pred[1280]{0:T(1024)(128)(4,1)S(1)} %broadcast_bitcast_fusion.3), kind=kOutput, calls=%fused_computation.16.clone.1 | convolution fusion | flops 348651520 | bytes 12338432 | tf_op jit(solution)/shard_map/while/body/eval_jaxpr/bhij,jhd->bihd/dot_general | solution.py:86
  91.2 3.0 %fusion.89 = (bf16[1280,512]{0,1:T(8,128)(2,1)S(1)}, bf16[1280,512]{0,1:T(8,128)(2,1)}) fusion(bf16[1280,1024]{0,1:T(8,128)(2,1)} %get-tuple-element.216), kind=kLoop, calls=%fused_computation.129.clone.1 | loop fusion | bytes 5242880 | tf_op jit(solution)/shard_map/while/body/eval_jaxpr/slice | solution.py:63
  99.4 6.5 %bitcast_reduce_fusion.2 = (f32[2,8,128]{2,0,1:T(2,128)S(1)}, f32[8,2,128,1280]{3,2,1,0:T(8,128)}) fusion(pred[1280]{0:T(1024)(128)(4,1)S(1)} %broadcast_bitcast_fusion.3, bf16[1280,8,64,1]{0,2,3,1:T(8,128)(2,1)S(1)} %bitcast.138, bf16[2,128,8,64]{1,0,3,2:T(2,128)(2,1)} %reshape.408), kind=kOutput, calls=%fused_computation.7.clone.1 | convolution fusion | flops 343406592 | bytes 12068096 | tf_op jit(solution)/shard_map/while/body/eval_jaxpr/bihd,jhd->bhij/dot_general | solution.py:73
  111.6 6.4 %fusion.93 = f32[2,8,128]{2,0,1:T(2,128)S(1)} fusion(f32[8,2,128,1280]{3,2,1,0:T(8,128)} %get-tuple-element.189, f32[2,8,128]{2,0,1:T(2,128)S(1)} %copy.190, pred[1280]{0:T(1024)(128)(4,1)S(1)} %broadcast_bitcast_fusion.3), kind=kLoop, calls=%fused_computation.11.clone.1 | loop fusion | flops 10483712 | bytes 10503424 | tf_op jit(solution)/shard_map/while/body/eval_jaxpr/reduce_sum | solution.py:80
  118.5 4.2 %fusion.94 = f32[2,128,8,64]{1,3,2,0:T(8,128)} fusion(bf16[1280,8,64,1]{0,2,1,3:T(8,128)(2,1)S(1)} %bitcast.140, f32[8,2,128,1280]{3,2,1,0:T(8,128)S(1)} %copy-done.1, f32[2,8,128]{2,0,1:T(2,128)S(1)} %copy.191, f32[2,8,128]{2,0,1:T(2,128)S(1)} %copy.190, pred[1280]{0:T(1024)(128)(4,1)S(1)} %broadcast_bitcast_fusion.3), kind=kOutput, calls=%fused_computation.16.clone.1 | convolution fusion | flops 348651520 | bytes 12338432 | tf_op jit(solution)/shard_map/while/body/eval_jaxpr/bhij,jhd->bihd/dot_general | solution.py:86
  128.0 3.0 %fusion.89 = (bf16[1280,512]{0,1:T(8,128)(2,1)S(1)}, bf16[1280,512]{0,1:T(8,128)(2,1)}) fusion(bf16[1280,1024]{0,1:T(8,128)(2,1)} %get-tuple-element.216), kind=kLoop, calls=%fused_computation.129.clone.1 | loop fusion | bytes 5242880 | tf_op jit(solution)/shard_map/while/body/eval_jaxpr/slice | solution.py:63
  136.2 6.5 %bitcast_reduce_fusion.2 = (f32[2,8,128]{2,0,1:T(2,128)S(1)}, f32[8,2,128,1280]{3,2,1,0:T(8,128)}) fusion(pred[1280]{0:T(1024)(128)(4,1)S(1)} %broadcast_bitcast_fusion.3, bf16[1280,8,64,1]{0,2,3,1:T(8,128)(2,1)S(1)} %bitcast.138, bf16[2,128,8,64]{1,0,3,2:T(2,128)(2,1)} %reshape.408), kind=kOutput, calls=%fused_computation.7.clone.1 | convolution fusion | flops 343406592 | bytes 12068096 | tf_op jit(solution)/shard_map/while/body/eval_jaxpr/bihd,jhd->bhij/dot_general | solution.py:73
  148.4 6.4 %fusion.93 = f32[2,8,128]{2,0,1:T(2,128)S(1)} fusion(f32[8,2,128,1280]{3,2,1,0:T(8,128)} %get-tuple-element.189, f32[2,8,128]{2,0,1:T(2,128)S(1)} %copy.190, pred[1280]{0:T(1024)(128)(4,1)S(1)} %broadcast_bitcast_fusion.3), kind=kLoop, calls=%fused_computation.11.clone.1 | loop fusion | flops 10483712 | bytes 10503424 | tf_op jit(solution)/shard_map/while/body/eval_jaxpr/reduce_sum | solution.py:80
  155.3 4.2 %fusion.94 = f32[2,128,8,64]{1,3,2,0:T(8,128)} fusion(bf16[1280,8,64,1]{0,2,1,3:T(8,128)(2,1)S(1)} %bitcast.140, f32[8,2,128,1280]{3,2,1,0:T(8,128)S(1)} %copy-done.1, f32[2,8,128]{2,0,1:T(2,128)S(1)} %copy.191, f32[2,8,128]{2,0,1:T(2,128)S(1)} %copy.190, pred[1280]{0:T(1024)(128)(4,1)S(1)} %broadcast_bitcast_fusion.3), kind=kOutput, calls=%fused_computation.16.clone.1 | convolution fusion | flops 348651520 | bytes 12338432 | tf_op jit(solution)/shard_map/while/body/eval_jaxpr/bhij,jhd->bihd/dot_general | solution.py:86
  173.0 6.5 %bitcast_reduce_fusion.2 = (f32[2,8,128]{2,0,1:T(2,128)S(1)}, f32[8,2,128,1280]{3,2,1,0:T(8,128)}) fusion(pred[1280]{0:T(1024)(128)(4,1)S(1)} %broadcast_bitcast_fusion.3, bf16[1280,8,64,1]{0,2,3,1:T(8,128)(2,1)S(1)} %bitcast.138, bf16[2,128,8,64]{1,0,3,2:T(2,128)(2,1)} %reshape.408), kind=kOutput, calls=%fused_computation.7.clone.1 | convolution fusion | flops 343406592 | bytes 12068096 | tf_op jit(solution)/shard_map/while/body/eval_jaxpr/bihd,jhd->bhij/dot_general | solution.py:73
  185.2 6.4 %fusion.93 = f32[2,8,128]{2,0,1:T(2,128)S(1)} fusion(f32[8,2,128,1280]{3,2,1,0:T(8,128)} %get-tuple-element.189, f32[2,8,128]{2,0,1:T(2,128)S(1)} %copy.190, pred[1280]{0:T(1024)(128)(4,1)S(1)} %broadcast_bitcast_fusion.3), kind=kLoop, calls=%fused_computation.11.clone.1 | loop fusion | flops 10483712 | bytes 10503424 | tf_op jit(solution)/shard_map/while/body/eval_jaxpr/reduce_sum | solution.py:80
  192.1 4.2 %fusion.94 = f32[2,128,8,64]{1,3,2,0:T(8,128)} fusion(bf16[1280,8,64,1]{0,2,1,3:T(8,128)(2,1)S(1)} %bitcast.140, f32[8,2,128,1280]{3,2,1,0:T(8,128)S(1)} %copy-done.1, f32[2,8,128]{2,0,1:T(2,128)S(1)} %copy.191, f32[2,8,128]{2,0,1:T(2,128)S(1)} %copy.190, pred[1280]{0:T(1024)(128)(4,1)S(1)} %broadcast_bitcast_fusion.3), kind=kOutput, calls=%fused_computation.16.clone.1 | convolution fusion | flops 348651520 | bytes 12338432 | tf_op jit(solution)/shard_map/while/body/eval_jaxpr/bhij,jhd->bihd/dot_general | solution.py:86
  205.7 8.3 %add_convert_fusion = bf16[1024,512]{0,1:T(8,128)(2,1)S(1)} fusion(f32[1024,512]{0,1:T(8,128)} %copy-done.6, bf16[2048,512]{1,0:T(8,128)(2,1)S(1)} %copy-done, bf16[512,2048]{1,0:T(8,128)(2,1)} %param.17, f32[512]{0:T(512)S(1)} %copy-done.13, f32[1024]{0:T(1024)S(1)} %add_rsqrt_fusion, f32[1024]{0:T(1024)S(1)} %broadcast_multiply_fusion), kind=kOutput, calls=%fused_computation.60 | convolution fusion | flops 4316987392 | bytes 7350272 | tf_op jit(solution)/shard_map/dot_general | solution.py:205
  (197 shorter events, 95.5 us)
Async XLA Ops:
  0.0 205.7 %copy-start = (bf16[2048,512]{1,0:T(8,128)(2,1)S(1)}, bf16[2048,512]{1,0:T(8,128)(2,1)}, u32[]{:S(2)}) copy-start(bf16[2048,512]{1,0:T(8,128)(2,1)} %param.18) | copy-start | bytes 6291460
  2.2 3.6 %copy-start.9 = (s32[32,10]{0,1:T(8,128)S(1)}, s32[32,10]{0,1:T(8,128)}, u32[]{:S(2)}) copy-start(s32[32,10]{0,1:T(8,128)} %param.21) | copy-start | bytes 3844
  6.1 10.8 %copy-start.7 = (bf16[1024,512]{1,0:T(8,128)(2,1)S(1)}, bf16[1024,512]{1,0:T(8,128)(2,1)}, u32[]{:S(2)}) copy-start(bf16[1024,512]{1,0:T(8,128)(2,1)} %copy.140) | copy-start | bytes 3145732
  9.0 33.2 %all-to-all-start = ((bf16[8,1,128,512]{3,2,1,0:T(8,128)(2,1)}), bf16[8,1,128,512]{3,2,1,0:T(8,128)(2,1)}, u32[]{:S(2)}, u32[]{:S(2)}) async-start(bf16[8,1,128,512]{3,2,1,0:T(8,128)(2,1)} %bitcast.145), calls=%async_computation | async-start | bytes 2097152 | tf_op jit(solution)/shard_map/all_to_all | solution.py:154
  19.4 13.0 %collective-permute-start.2 = (bf16[1,1,128,512]{3,2,1,0:T(8,128)(2,1)S(1)}, bf16[1,1,128,512]{3,2,1,0:T(8,128)(2,1)S(1)}, u32[]{:S(2)}, u32[]{:S(2)}) collective-permute-start(bf16[1,1,128,512]{3,2,1,0:T(8,128)(2,1)S(1)} %get-tuple-element.127), channel_id=1, source_target_pairs={{0,24},{8,16},{16,8},{24,0},{1,25},{9,17},{17,9},{25,1},{2,26},{10... | collective-permute-start | bytes 393224 | tf_op jit(solution)/shard_map/ppermute | solution.py:39
  20.1 12.3 %collective-permute-start.1 = (bf16[1,1,128,512]{3,2,1,0:T(8,128)(2,1)S(1)}, bf16[1,1,128,512]{3,2,1,0:T(8,128)(2,1)S(1)}, u32[]{:S(2)}, u32[]{:S(2)}) collective-permute-start(bf16[1,1,128,512]{3,2,1,0:T(8,128)(2,1)S(1)} %get-tuple-element.125), channel_id=1, source_target_pairs={{0,16},{8,24},{16,0},{24,8},{1,17},{9,25},{17,1},{25,9},{2,18},{10... | collective-permute-start | bytes 393224 | tf_op jit(solution)/shard_map/ppermute | solution.py:39
  21.0 11.4 %collective-permute-start = (bf16[1,1,128,512]{3,2,1,0:T(8,128)(2,1)S(1)}, bf16[1,1,128,512]{3,2,1,0:T(8,128)(2,1)S(1)}, u32[]{:S(2)}, u32[]{:S(2)}) collective-permute-start(bf16[1,1,128,512]{3,2,1,0:T(8,128)(2,1)S(1)} %get-tuple-element.126), channel_id=1, source_target_pairs={{0,8},{8,0},{16,24},{24,16},{1,9},{9,1},{17,25},{25,17},{2,10},{10... | collective-permute-start | bytes 393224 | tf_op jit(solution)/shard_map/ppermute | solution.py:39
  34.9 10.3 %copy-start.8 = (bf16[10,128,512]{2,1,0:T(8,128)(2,1)S(1)}, bf16[10,128,512]{2,1,0:T(8,128)(2,1)}, u32[]{:S(2)}) copy-start(bf16[10,128,512]{2,1,0:T(8,128)(2,1)} %gather_fusion.4) | copy-start | bytes 3932164
  69.2 4.0 %copy-start.2 = (bf16[2,128,8,64]{1,0,3,2:T(2,128)(2,1)S(1)}, bf16[2,128,8,64]{1,0,3,2:T(2,128)(2,1)}, u32[]{:S(2)}) copy-start(bf16[2,128,8,64]{1,0,3,2:T(2,128)(2,1)} %reshape.408) | copy-start | bytes 786436 | tf_op jit(solution)/shard_map/while
  73.2 8.0 %copy-start.3 = (bf16[1280,512]{0,1:T(8,128)(2,1)S(1)}, bf16[1280,512]{0,1:T(8,128)(2,1)}, u32[]{:S(2)}) copy-start(bf16[1280,512]{0,1:T(8,128)(2,1)} %get-tuple-element.187) | copy-start | bytes 3932164 | tf_op jit(solution)/shard_map/while
  74.8 7.0 %copy-start.1 = (f32[8,2,128,1280]{3,2,1,0:T(8,128)S(1)}, f32[8,2,128,1280]{3,2,1,0:T(8,128)}, u32[]{:S(2)}) copy-start(f32[8,2,128,1280]{3,2,1,0:T(8,128)} %get-tuple-element.189) | copy-start | bytes 31457284 | tf_op jit(solution)/shard_map/while
  81.7 4.2 %copy-start.5 = (bf16[256,512]{0,1:T(8,128)(2,1)S(1)}, bf16[256,512]{0,1:T(8,128)(2,1)}, u32[]{:S(2)}) copy-start(bf16[256,512]{0,1:T(8,128)(2,1)} %get-tuple-element.194) | copy-start | bytes 786436 | tf_op jit(solution)/shard_map/while
  106.0 4.0 %copy-start.2 = (bf16[2,128,8,64]{1,0,3,2:T(2,128)(2,1)S(1)}, bf16[2,128,8,64]{1,0,3,2:T(2,128)(2,1)}, u32[]{:S(2)}) copy-start(bf16[2,128,8,64]{1,0,3,2:T(2,128)(2,1)} %reshape.408) | copy-start | bytes 786436 | tf_op jit(solution)/shard_map/while
  110.0 8.1 %copy-start.3 = (bf16[1280,512]{0,1:T(8,128)(2,1)S(1)}, bf16[1280,512]{0,1:T(8,128)(2,1)}, u32[]{:S(2)}) copy-start(bf16[1280,512]{0,1:T(8,128)(2,1)} %get-tuple-element.187) | copy-start | bytes 3932164 | tf_op jit(solution)/shard_map/while
  111.6 7.0 %copy-start.1 = (f32[8,2,128,1280]{3,2,1,0:T(8,128)S(1)}, f32[8,2,128,1280]{3,2,1,0:T(8,128)}, u32[]{:S(2)}) copy-start(f32[8,2,128,1280]{3,2,1,0:T(8,128)} %get-tuple-element.189) | copy-start | bytes 31457284 | tf_op jit(solution)/shard_map/while
  118.5 4.2 %copy-start.5 = (bf16[256,512]{0,1:T(8,128)(2,1)S(1)}, bf16[256,512]{0,1:T(8,128)(2,1)}, u32[]{:S(2)}) copy-start(bf16[256,512]{0,1:T(8,128)(2,1)} %get-tuple-element.194) | copy-start | bytes 786436 | tf_op jit(solution)/shard_map/while
  142.8 4.0 %copy-start.2 = (bf16[2,128,8,64]{1,0,3,2:T(2,128)(2,1)S(1)}, bf16[2,128,8,64]{1,0,3,2:T(2,128)(2,1)}, u32[]{:S(2)}) copy-start(bf16[2,128,8,64]{1,0,3,2:T(2,128)(2,1)} %reshape.408) | copy-start | bytes 786436 | tf_op jit(solution)/shard_map/while
  146.7 8.1 %copy-start.3 = (bf16[1280,512]{0,1:T(8,128)(2,1)S(1)}, bf16[1280,512]{0,1:T(8,128)(2,1)}, u32[]{:S(2)}) copy-start(bf16[1280,512]{0,1:T(8,128)(2,1)} %get-tuple-element.187) | copy-start | bytes 3932164 | tf_op jit(solution)/shard_map/while
  148.4 7.0 %copy-start.1 = (f32[8,2,128,1280]{3,2,1,0:T(8,128)S(1)}, f32[8,2,128,1280]{3,2,1,0:T(8,128)}, u32[]{:S(2)}) copy-start(f32[8,2,128,1280]{3,2,1,0:T(8,128)} %get-tuple-element.189) | copy-start | bytes 31457284 | tf_op jit(solution)/shard_map/while
  155.3 4.2 %copy-start.5 = (bf16[256,512]{0,1:T(8,128)(2,1)S(1)}, bf16[256,512]{0,1:T(8,128)(2,1)}, u32[]{:S(2)}) copy-start(bf16[256,512]{0,1:T(8,128)(2,1)} %get-tuple-element.194) | copy-start | bytes 786436 | tf_op jit(solution)/shard_map/while
  179.6 4.0 %copy-start.2 = (bf16[2,128,8,64]{1,0,3,2:T(2,128)(2,1)S(1)}, bf16[2,128,8,64]{1,0,3,2:T(2,128)(2,1)}, u32[]{:S(2)}) copy-start(bf16[2,128,8,64]{1,0,3,2:T(2,128)(2,1)} %reshape.408) | copy-start | bytes 786436 | tf_op jit(solution)/shard_map/while
  183.5 8.1 %copy-start.3 = (bf16[1280,512]{0,1:T(8,128)(2,1)S(1)}, bf16[1280,512]{0,1:T(8,128)(2,1)}, u32[]{:S(2)}) copy-start(bf16[1280,512]{0,1:T(8,128)(2,1)} %get-tuple-element.187) | copy-start | bytes 3932164 | tf_op jit(solution)/shard_map/while
  185.2 7.0 %copy-start.1 = (f32[8,2,128,1280]{3,2,1,0:T(8,128)S(1)}, f32[8,2,128,1280]{3,2,1,0:T(8,128)}, u32[]{:S(2)}) copy-start(f32[8,2,128,1280]{3,2,1,0:T(8,128)} %get-tuple-element.189) | copy-start | bytes 31457284 | tf_op jit(solution)/shard_map/while
  192.1 4.2 %copy-start.5 = (bf16[256,512]{0,1:T(8,128)(2,1)S(1)}, bf16[256,512]{0,1:T(8,128)(2,1)}, u32[]{:S(2)}) copy-start(bf16[256,512]{0,1:T(8,128)(2,1)} %get-tuple-element.194) | copy-start | bytes 786436 | tf_op jit(solution)/shard_map/while
  (6 other events, 12.5 us)
